TPU v7x, 256 devices: a whole 4x4x8 slice. The times are simulated.
256 devices in a mesh: seq: 32 (over z, x), head: 8 (over y, core).
Axes of the slice: x: 4, y: 4, z: 8, core: 2. Of those that a mesh axis runs over, the one named last changes fastest.
Arguments:
- queries: bfloat16 [8192, 1024], P('seq', 'head'), may hold values from -16 to 16
- keys: bfloat16 [8192, 1024], P(('seq', 'head')), may hold values from -16 to 16
- values: bfloat16 [8192, 1024], P(('seq', 'head')), may hold values from -6 to 6
- out_grad: bfloat16 [8192, 1024], P('seq', 'head'), may hold values from -6 to 6
Outputs:
- attended: bfloat16 [8192, 1024], P('seq', 'head')
- query_grad: float32 [8192, 1024], P('seq', 'head')
- key_grad: float32 [8192, 1024], P('seq', 'head')
- value_grad: float32 [8192, 1024], P('seq', 'head')
All inputs are finite; a program needn't handle non-finite values.
Results may differ from a plain program's by a relative error of at most 0.0095.
Values may be sent and summed in bfloat16 or wider, within the bound.
No kernel may reach another device: no remote copies, remote signals or barrier semaphores. Data moves between devices by JAX's collectives and lax.ppermute only.
A program may use at most 64 MiB of HBM per device.

v0:
```python
import math
import jax
import jax.numpy as jnp
from jax import lax
from jax.sharding import Mesh
from jax.sharding import PartitionSpec as P

SEQ = ("seq_0", "seq_1")
SEQ_HEAD = ("seq_0", "seq_1", "head")
masked_value = -1e30


def whole_of(array, axes, dim):
    filled = array
    for number in range(len(axes) - 1, -1, -1):
        filled = lax.all_gather(filled, axes[number], axis=dim, tiled=True)
    return filled


def joined_along(parts, dim):
    dims = list(parts.shape[1:])
    dims[dim] *= parts.shape[0]
    return jnp.moveaxis(parts, 0, dim).reshape(dims)


def gather_packed(arrays, axis, dims):
    ravelled = jnp.concatenate([a.reshape(-1) for a in arrays])
    lines, at, gathered = (lax.all_gather(ravelled, axis), 0, [])
    for a, dim in zip(arrays, dims):
        parts = lines[:, at : at + a.size].reshape(-1, *a.shape)
        gathered.append(joined_along(parts, dim))
        at += a.size
    return tuple(gathered)


def key_block(length, row_count):
    return min(length, max(1024, 2 * row_count))


def attend_range(queries, qstart, whole_keys, whole_values, key_low, key_high, scaling):
    row_count, head_width = queries.shape
    length = whole_keys.shape[0]
    span_rows = key_block(length, row_count)
    query_pos = qstart + jnp.arange(row_count, dtype=jnp.int32)

    def attend_compute(running, kstart):
        weighted, rowmax, rowsum = running
        key_piece = lax.dynamic_slice_in_dim(whole_keys, kstart, span_rows, 0)
        value_piece = lax.dynamic_slice_in_dim(whole_values, kstart, span_rows, 0)
        key_pos = kstart + jnp.arange(span_rows, dtype=jnp.int32)
        allowed = (
            (key_pos[None, :] <= query_pos[:, None])
            & (key_pos[None, :] >= key_low)
            & (key_pos[None, :] < key_high)
        )
        scores = (
            jnp.einsum("qd,kd->qk", queries, key_piece, preferred_element_type=jnp.float32)
            * scaling
        )
        scores = jnp.where(allowed, scores, masked_value)
        new_max = jnp.maximum(rowmax, jnp.max(scores, axis=1))
        weights = jnp.where(allowed, jnp.exp(scores - new_max[:, None]), 0.0)
        factor = jnp.exp(rowmax - new_max)
        rowsum = rowsum * factor + jnp.sum(weights, axis=1)
        weighted = weighted * factor[:, None] + jnp.dot(
            weights.astype(jnp.bfloat16), value_piece, preferred_element_type=jnp.float32
        )
        return (weighted, new_max, rowsum)

    def attend_advance(counter, running):
        kstart = counter * span_rows
        needed = (
            (kstart < key_high) & (kstart + span_rows > key_low) & (kstart < qstart + row_count)
        )
        return lax.cond(
            needed,
            lambda previous: attend_compute(previous, kstart),
            lambda previous: previous,
            running,
        )

    initial = (
        jnp.zeros((row_count, head_width), jnp.float32),
        jnp.full((row_count,), masked_value, jnp.float32),
        jnp.zeros((row_count,), jnp.float32),
    )
    return lax.fori_loop(0, length // span_rows, attend_advance, initial)


def backward_range(
    queries,
    out_grad,
    log_norm,
    row_delta,
    qstart,
    whole_keys,
    whole_values,
    key_low,
    key_high,
    scaling,
):
    row_count, head_width = queries.shape
    length = whole_keys.shape[0]
    span_rows = key_block(length, row_count)
    query_pos = qstart + jnp.arange(row_count, dtype=jnp.int32)

    def backward_compute(running, kstart):
        query_part, terms = running
        key_piece = lax.dynamic_slice_in_dim(whole_keys, kstart, span_rows, 0)
        value_piece = lax.dynamic_slice_in_dim(whole_values, kstart, span_rows, 0)
        key_pos = kstart + jnp.arange(span_rows, dtype=jnp.int32)
        allowed = (
            (key_pos[None, :] <= query_pos[:, None])
            & (key_pos[None, :] >= key_low)
            & (key_pos[None, :] < key_high)
        )
        scores = (
            jnp.einsum("qd,kd->qk", queries, key_piece, preferred_element_type=jnp.float32)
            * scaling
        )
        probs = jnp.where(allowed, jnp.exp(scores - log_norm[:, None]), 0.0)
        grad_probs = jnp.einsum(
            "qd,kd->qk", out_grad, value_piece, preferred_element_type=jnp.float32
        )
        grad_scores = (probs * (grad_probs - row_delta[:, None]) * scaling).astype(jnp.bfloat16)
        query_part = query_part + jnp.dot(
            grad_scores, key_piece, preferred_element_type=jnp.float32
        )
        return (query_part, terms)

    def backward_advance(counter, running):
        kstart = counter * span_rows
        needed = (
            (kstart < key_high) & (kstart + span_rows > key_low) & (kstart < qstart + row_count)
        )
        return lax.cond(
            needed,
            lambda previous: backward_compute(previous, kstart),
            lambda previous: previous,
            running,
        )

    initial = (jnp.zeros((row_count, head_width), jnp.float32), None)
    return lax.fori_loop(0, length // span_rows, backward_advance, initial)


def key_range(all_rows, all_grads, all_norms, all_deltas, own_keys, own_values, kstart, scaling):
    length = all_rows.shape[0]
    row_count, head_width = own_keys.shape
    span_rows = key_block(length, row_count)
    key_pos = kstart + jnp.arange(row_count, dtype=jnp.int32)

    def key_compute(running, qstart):
        key_total, value_total = running
        query_piece = lax.dynamic_slice_in_dim(all_rows, qstart, span_rows, 0)
        grad_piece = lax.dynamic_slice_in_dim(all_grads, qstart, span_rows, 0)
        norm_piece = lax.dynamic_slice_in_dim(all_norms, qstart, span_rows, 0)
        delta_piece = lax.dynamic_slice_in_dim(all_deltas, qstart, span_rows, 0)
        query_pos = qstart + jnp.arange(span_rows, dtype=jnp.int32)
        allowed = key_pos[None, :] <= query_pos[:, None]
        scores = (
            jnp.einsum("qd,kd->qk", query_piece, own_keys, preferred_element_type=jnp.float32)
            * scaling
        )
        probs = jnp.where(allowed, jnp.exp(scores - norm_piece[:, None]), 0.0)
        grad_probs = jnp.einsum(
            "qd,kd->qk", grad_piece, own_values, preferred_element_type=jnp.float32
        )
        grad_scores = (probs * (grad_probs - delta_piece[:, None]) * scaling).astype(jnp.bfloat16)
        key_total = key_total + jnp.einsum(
            "qk,qd->kd", grad_scores, query_piece, preferred_element_type=jnp.float32
        )
        value_total = value_total + jnp.einsum(
            "qk,qd->kd", probs.astype(jnp.bfloat16), grad_piece, preferred_element_type=jnp.float32
        )
        return (key_total, value_total)

    def key_advance(counter, running):
        qstart = counter * span_rows
        needed = qstart + span_rows > kstart
        return lax.cond(
            needed,
            lambda previous: key_compute(previous, qstart),
            lambda previous: previous,
            running,
        )

    initial = (
        jnp.zeros((row_count, head_width), jnp.float32),
        jnp.zeros((row_count, head_width), jnp.float32),
    )
    return lax.fori_loop(0, length // span_rows, key_advance, initial)


def per_device(queries, keys, values, out_grad):
    row_count, head_width = queries.shape
    scaling = 1.0 / math.sqrt(head_width)
    local_keys, local_values = (
        lax.all_to_all(keys, "head", split_axis=1, concat_axis=0, tiled=True),
        lax.all_to_all(values, "head", split_axis=1, concat_axis=0, tiled=True),
    )
    whole_keys, whole_values = (whole_of(local_keys, SEQ, 0), whole_of(local_values, SEQ, 0))
    length = whole_keys.shape[0]
    device = lax.axis_index(SEQ)
    qstart = device * row_count
    weighted, rowmax, rowsum = attend_range(
        queries, qstart, whole_keys, whole_values, 0, length, scaling
    )
    output = weighted / rowsum[:, None]
    log_norm = rowmax + jnp.log(rowsum)
    attended = output.astype(jnp.bfloat16)
    row_delta = jnp.sum(out_grad.astype(jnp.float32) * output, axis=1)
    query_grad, unused = backward_range(
        queries, out_grad, log_norm, row_delta, qstart, whole_keys, whole_values, 0, length, scaling
    )
    all_rows, all_grads = (whole_of(queries, SEQ, 0), whole_of(out_grad, SEQ, 0))
    all_norms, all_deltas = gather_packed((log_norm, row_delta), SEQ, (0, 0))
    key_grad, value_grad = key_range(
        all_rows, all_grads, all_norms, all_deltas, local_keys, local_values, qstart, scaling
    )
    return (attended, query_grad, key_grad, value_grad)


def solution(mesh):
    split = Mesh(mesh.devices.reshape(8, 4, mesh.shape["head"]), ("seq_0", "seq_1", "head"))
    return jax.shard_map(
        per_device,
        mesh=split,
        in_specs=(P(SEQ, "head"), P(SEQ_HEAD, None), P(SEQ_HEAD, None), P(SEQ, "head")),
        out_specs=(P(SEQ, "head"), P(SEQ, "head"), P(SEQ, "head"), P(SEQ, "head")),
        check_vma=False,
    )
```

profile of v0, /device:TPU:8, one launch (start us, length us, event | category | flops | bytes accessed | tf_op | source)
XLA Modules:
  0.0 247.4 jit_solution(4875026922688107261)
XLA Ops:
  8.0 8.9 %all_to_all.38 = bf16[32,8,128]{2,0,1:T(8,128)(2,1)S(1)} all-to-all(bf16[32,8,128]{2,0,1:T(8,128)(2,1)S(1)} %copy_bitcast_fusion.1), channel_id=1, replica_groups=mesh['seq_0'=8,'seq_1'=4,'head'=8] {'head'}, dimensions={1} | all-to-all | bytes 131072 | tf_op jit(solution)/shard_map/all_to_all | solution.py:199
  16.9 13.3 %all_gather.30 = bf16[1024,128]{1,0:T(8,128)(2,1)} all-gather(bf16[256,128]{1,0:T(8,128)(2,1)S(1)} %bitcast.53), channel_id=1, replica_groups=mesh['seq_0'=8,'seq_1'=4,'head'=8] {'seq_1'}, dimensions={0}, use_global_device_ids=true | all-gather | bytes 327680 | tf_op jit(solution)/shard_map/all_gather | solution.py:16
  31.2 8.0 %all_to_all.39 = bf16[32,8,128]{2,0,1:T(8,128)(2,1)S(1)} all-to-all(bf16[32,8,128]{2,0,1:T(8,128)(2,1)S(1)} %copy_bitcast_fusion), channel_id=1, replica_groups=mesh['seq_0'=8,'seq_1'=4,'head'=8] {'head'}, dimensions={1} | all-to-all | bytes 131072 | tf_op jit(solution)/shard_map/all_to_all | solution.py:200
  39.2 13.0 %all_gather.32 = bf16[1024,128]{1,0:T(8,128)(2,1)} all-gather(bf16[256,128]{1,0:T(8,128)(2,1)S(1)} %bitcast.51), channel_id=1, replica_groups=mesh['seq_0'=8,'seq_1'=4,'head'=8] {'seq_1'}, dimensions={0}, use_global_device_ids=true | all-gather | bytes 327680 | tf_op jit(solution)/shard_map/all_gather | solution.py:16
  52.2 14.0 %all_gather.34 = bf16[1024,128]{1,0:T(8,128)(2,1)} all-gather(bf16[256,128]{1,0:T(8,128)(2,1)} %param.16), channel_id=1, replica_groups=mesh['seq_0'=8,'seq_1'=4,'head'=8] {'seq_1'}, dimensions={0}, use_global_device_ids=true | all-gather | bytes 327680 | tf_op jit(solution)/shard_map/all_gather | solution.py:16
  66.4 13.1 %all_gather.38 = bf16[1024,128]{1,0:T(8,128)(2,1)} all-gather(bf16[256,128]{1,0:T(8,128)(2,1)S(1)} %copy-done.4), channel_id=1, replica_groups=mesh['seq_0'=8,'seq_1'=4,'head'=8] {'seq_1'}, dimensions={0}, use_global_device_ids=true | all-gather | bytes 327680 | tf_op jit(solution)/shard_map/all_gather | solution.py:16
  79.5 34.4 %all-gather.9.cloned.1.call-done = bf16[8192,128]{1,0:T(8,128)(2,1)} async-done(((bf16[1024,128]{1,0:T(8,128)(2,1)}), bf16[8192,128]{1,0:T(8,128)(2,1)}) %all-gather.9.cloned.1.call-update) | async-done | bytes 2097168 | tf_op jit(solution)/shard_map/all_gather | solution.py:16
  113.9 5.1 %while.56 = (s32[]{:T(128)}, f32[256,128]{1,0:T(8,128)S(1)}, f32[256]{0:T(256)S(1)}, f32[256]{0:T(256)S(1)}, s32[]{:T(128)}, /*index=5*/bf16[8192,128]{1,0:T(8,1...) while((s32[]{:T(128)}, f32[256,128]{1,0:T(8,128)S(1)}, ...), condition=%wide.region_5.6_spmd.clone, body=%wide.region_0.5_spmd.clone.sunk | while | flops 139006736 | bytes 4045177 | solution.py:87
  114.0 4.6 %conditional.10 = ((f32[256,128]{1,0:T(8,128)S(1)}, f32[256]{0:T(256)S(1)}, f32[256]{0:T(256)S(1)})) conditional(s32[]{:T(128)} %convert_element_type.68, (f32[256,128]{1,0:T(8,128)S(1)}, f32[256]{0:T(256)S(1)}, f32[256]{0:T(256)S(1)}) %tuple.146, (s32[]{:T(128)}, s32[]{:T(128)}, bf16[8192,128]{1,0:T(8,128)(2,1)}, bf16[256,128]{1,0:T(8,128)(2,1)S(1)}, ...), branch_computations={%region_1.0_spmd, %region_2.4_spmd} | conditional | flops 139006720 | bytes 4043862 | solution.py:75
  114.1 1.9 fusion.68
  116.8 1.8 convolution_add_fusion
  119.8 80.2 %all-gather.1 = f32[32,1,512]{2,1,0:T(1,128)S(1)} all-gather(f32[1,1,512]{2,1,0:T(1,128)S(1)} %bitcast.58), channel_id=2, replica_groups=mesh['seq_0'=8,'seq_1'=4,'head'=8] {'seq_0','seq_1'}, dimensions={0}, use_global_device_ids=true | all-gather | bytes 67584 | tf_op jit(solution)/shard_map/all_gather | solution.py:28
  200.1 3.5 %while.57 = (s32[]{:T(128)}, f32[256,128]{1,0:T(8,128)S(1)}, s32[]{:T(128)}, bf16[8192,128]{1,0:T(8,128)(2,1)}, bf16[256,128]{1,0:T(8,128)(2,1)S(1)}, /*index=5*...) while((s32[]{:T(128)}, f32[256,128]{1,0:T(8,128)S(1)}, ...), condition=%wide.region_10.11_spmd.clone, body=%wide.region_7.10_spmd.clone.sunk | while | flops 203985168 | bytes 3296597 | solution.py:144
  200.2 3.0 %conditional.11 = (f32[256,128]{1,0:T(8,128)S(1)}) conditional(s32[]{:T(128)} %convert_element_type.69, f32[256,128]{1,0:T(8,128)S(1)} %get-tuple-element.1194, (s32[]{:T(128)}, s32[]{:T(128)}, bf16[8192,128]{1,0:T(8,128)(2,1)}, bf16[256,128]{1,0:T(8,128)(2,1)S(1)}, f32[256]{0:T(256)S(1)}, /*index=5*/bf16[8192,128]{1,0:T(8,128)(2,1)}, ...), branch_computations={%region_8.8_spmd, %region_9.9_spmd} | conditional | flops 203985152 | bytes 3295290 | solution.py:136
  204.3 35.9 %while.58 = (s32[]{:T(128)}, f32[256,128]{1,0:T(8,128)S(1)}, f32[256,128]{1,0:T(8,128)S(1)}, s32[]{:T(128)}, bf16[8192,128]{1,0:T(8,128)(2,1)}, /*index=5*/bf16[...) while((s32[]{:T(128)}, f32[256,128]{1,0:T(8,128)S(1)}, ...), condition=%wide.region_14.15_spmd.clone.clone, body=%wide.region_11.14_spmd.clone.clone.sunk | while | flops 270861568 | bytes 4887901 | solution.py:192
  204.3 4.4 %conditional.12 = ((f32[256,128]{1,0:T(8,128)S(1)}, f32[256,128]{1,0:T(8,128)S(1)})) conditional(s32[]{:T(128)} %convert_element_type.70, (f32[256,128]{1,0:T(8,128)S(1)}, f32[256,128]{1,0:T(8,128)S(1)}) %tuple.151, (s32[]{:T(128)}, s32[]{:T(128)}, bf16[8192,128]{1,0:T(8,128)(2,1)}, bf16[256,128]{1,0:T(8,128)(2,1)S(1)}, f32[8192]{0:T(1024)S(1)}, ...), branch_computations={%region_12.12_spmd, %region_13.13_spmd} | conditional | flops 270861568 | bytes 4886610 | solution.py:181
  208.7 4.5 %conditional.12 = ((f32[256,128]{1,0:T(8,128)S(1)}, f32[256,128]{1,0:T(8,128)S(1)})) conditional(s32[]{:T(128)} %convert_element_type.70, (f32[256,128]{1,0:T(8,128)S(1)}, f32[256,128]{1,0:T(8,128)S(1)}) %tuple.151, (s32[]{:T(128)}, s32[]{:T(128)}, bf16[8192,128]{1,0:T(8,128)(2,1)}, bf16[256,128]{1,0:T(8,128)(2,1)S(1)}, f32[8192]{0:T(1024)S(1)}, ...), branch_computations={%region_12.12_spmd, %region_13.13_spmd} | conditional | flops 270861568 | bytes 4886610 | solution.py:181
  210.2 1.7 fusion.53
  213.2 4.5 %conditional.12 = ((f32[256,128]{1,0:T(8,128)S(1)}, f32[256,128]{1,0:T(8,128)S(1)})) conditional(s32[]{:T(128)} %convert_element_type.70, (f32[256,128]{1,0:T(8,128)S(1)}, f32[256,128]{1,0:T(8,128)S(1)}) %tuple.151, (s32[]{:T(128)}, s32[]{:T(128)}, bf16[8192,128]{1,0:T(8,128)(2,1)}, bf16[256,128]{1,0:T(8,128)(2,1)S(1)}, f32[8192]{0:T(1024)S(1)}, ...), branch_computations={%region_12.12_spmd, %region_13.13_spmd} | conditional | flops 270861568 | bytes 4886610 | solution.py:181
  217.7 4.5 %conditional.12 = ((f32[256,128]{1,0:T(8,128)S(1)}, f32[256,128]{1,0:T(8,128)S(1)})) conditional(s32[]{:T(128)} %convert_element_type.70, (f32[256,128]{1,0:T(8,128)S(1)}, f32[256,128]{1,0:T(8,128)S(1)}) %tuple.151, (s32[]{:T(128)}, s32[]{:T(128)}, bf16[8192,128]{1,0:T(8,128)(2,1)}, bf16[256,128]{1,0:T(8,128)(2,1)S(1)}, f32[8192]{0:T(1024)S(1)}, ...), branch_computations={%region_12.12_spmd, %region_13.13_spmd} | conditional | flops 270861568 | bytes 4886610 | solution.py:181
  222.2 4.5 %conditional.12 = ((f32[256,128]{1,0:T(8,128)S(1)}, f32[256,128]{1,0:T(8,128)S(1)})) conditional(s32[]{:T(128)} %convert_element_type.70, (f32[256,128]{1,0:T(8,128)S(1)}, f32[256,128]{1,0:T(8,128)S(1)}) %tuple.151, (s32[]{:T(128)}, s32[]{:T(128)}, bf16[8192,128]{1,0:T(8,128)(2,1)}, bf16[256,128]{1,0:T(8,128)(2,1)S(1)}, f32[8192]{0:T(1024)S(1)}, ...), branch_computations={%region_12.12_spmd, %region_13.13_spmd} | conditional | flops 270861568 | bytes 4886610 | solution.py:181
  226.7 4.5 %conditional.12 = ((f32[256,128]{1,0:T(8,128)S(1)}, f32[256,128]{1,0:T(8,128)S(1)})) conditional(s32[]{:T(128)} %convert_element_type.70, (f32[256,128]{1,0:T(8,128)S(1)}, f32[256,128]{1,0:T(8,128)S(1)}) %tuple.151, (s32[]{:T(128)}, s32[]{:T(128)}, bf16[8192,128]{1,0:T(8,128)(2,1)}, bf16[256,128]{1,0:T(8,128)(2,1)S(1)}, f32[8192]{0:T(1024)S(1)}, ...), branch_computations={%region_12.12_spmd, %region_13.13_spmd} | conditional | flops 270861568 | bytes 4886610 | solution.py:181
  231.2 4.5 %conditional.12 = ((f32[256,128]{1,0:T(8,128)S(1)}, f32[256,128]{1,0:T(8,128)S(1)})) conditional(s32[]{:T(128)} %convert_element_type.70, (f32[256,128]{1,0:T(8,128)S(1)}, f32[256,128]{1,0:T(8,128)S(1)}) %tuple.151, (s32[]{:T(128)}, s32[]{:T(128)}, bf16[8192,128]{1,0:T(8,128)(2,1)}, bf16[256,128]{1,0:T(8,128)(2,1)S(1)}, f32[8192]{0:T(1024)S(1)}, ...), branch_computations={%region_12.12_spmd, %region_13.13_spmd} | conditional | flops 270861568 | bytes 4886610 | solution.py:181
  235.7 4.5 %conditional.12 = ((f32[256,128]{1,0:T(8,128)S(1)}, f32[256,128]{1,0:T(8,128)S(1)})) conditional(s32[]{:T(128)} %convert_element_type.70, (f32[256,128]{1,0:T(8,128)S(1)}, f32[256,128]{1,0:T(8,128)S(1)}) %tuple.151, (s32[]{:T(128)}, s32[]{:T(128)}, bf16[8192,128]{1,0:T(8,128)(2,1)}, bf16[256,128]{1,0:T(8,128)(2,1)S(1)}, f32[8192]{0:T(1024)S(1)}, ...), branch_computations={%region_12.12_spmd, %region_13.13_spmd} | conditional | flops 270861568 | bytes 4886610 | solution.py:181
  (143 shorter events, 41.5 us)
Async XLA Ops:
  7.2 0.8 copy-start
  7.2 106.8 %copy-start.5 = (bf16[256,128]{1,0:T(8,128)(2,1)S(1)}, bf16[256,128]{1,0:T(8,128)(2,1)}, u32[]{:S(2)}) copy-start(bf16[256,128]{1,0:T(8,128)(2,1)} %param.16) | copy-start | bytes 196612
  7.2 59.2 %copy-start.4 = (bf16[256,128]{1,0:T(8,128)(2,1)S(1)}, bf16[256,128]{1,0:T(8,128)(2,1)}, u32[]{:S(2)}) copy-start(bf16[256,128]{1,0:T(8,128)(2,1)} %param.19) | copy-start | bytes 196612
  7.2 72.3 %all-gather.7.cloned.1.call-start = ((), (), s32[]{:S(2)}) async-start(), calls=%async_computation.2 | async-start | bytes 2359296 | tf_op jit(solution)/shard_map/all_gather | solution.py:16
  30.3 83.6 %all-gather.9.cloned.1.call-start = ((), (), s32[]{:S(2)}) async-start(), calls=%async_computation.3 | async-start | bytes 2359296 | tf_op jit(solution)/shard_map/all_gather | solution.py:16
  52.2 151.4 %all-gather.11.cloned.1.call-start = ((), (), s32[]{:S(2)}) async-start(), calls=%async_computation.4 | async-start | bytes 2359296 | tf_op jit(solution)/shard_map/all_gather | solution.py:16
  66.3 137.4 %all-gather.13.cloned.1.call-start = ((), (), s32[]{:S(2)}) async-start(), calls=%async_computation.5 | async-start | bytes 2359296 | tf_op jit(solution)/shard_map/all_gather | solution.py:16
  203.6 0.7 copy-start.3
  240.2 0.7 copy-start.1
  240.2 0.7 copy-start.2
Sparse Core Ops, SparseCore 0:
  30.4 42.2 all-gather.6
  74.5 39.4 all-gather.8
  115.7 39.4 all-gather.10
  156.8 39.5 all-gather.12
where the time goes:
time: 249 us; the launch traced here: 247 us
  blocking collectives  151 us (61%)
  matrix products  41.4 us (17%)
  waiting for transfers between devices  34.5 us (14%)
  between operations  14 us (6%)
  local copies, waits for them, and re-layouts  3.2 us (1%)
    all_gather x1, blocking collectives, gather_packed(): lines, at, gathered = (lax.all_gather(ravelled, axis), 0, [])  80.2 us
    all_gather x4, blocking collectives, whole_of(): filled = lax.all_gather(filled, axes[number], axis=dim, tiled=True)  53.5 us
    all_gather x4, waiting for transfers between devices, whole_of(): filled = lax.all_gather(filled, axes[number], axis=dim, tiled=True)  34.4 us
    dot_general x8, matrix products, key_compute(): jnp.einsum('qk,qd->kd', grad_scores, query_piece, preferred_element_type=...  13.6 us
    dot_general x8, matrix products, key_compute(): jnp.einsum('qd,kd->qk', query_piece, own_keys, preferred_element_type=jnp...  10.8 us
    dot_general x8, matrix products, key_compute(): jnp.einsum('qk,qd->kd', probs.astype(jnp.bfloat16), grad_piece, preferred...  10.4 us
    all_to_all x1, blocking collectives, per_device(): lax.all_to_all(keys, 'head', split_axis=1, concat_axis=0, tiled=True)  8.88 us
    all_to_all x1, blocking collectives, per_device(): lax.all_to_all(values, 'head', split_axis=1, concat_axis=0, tiled=True)  8 us
  transfers between devices with their start and end apart: 4, of which 1 were waited for; matrix products, arithmetic and copies ran while one was open for 4% of the time, Pallas kernels for 0%

commit v1 on v0

--- a/solution.py
+++ b/solution.py
@@ -196,7 +196,10 @@
     row_count, head_width = queries.shape
     scaling = 1.0 / math.sqrt(head_width)
     local_keys, local_values = (
-        lax.all_to_all(keys, "head", split_axis=1, concat_axis=0, tiled=True),
+        jnp.concatenate(
+            lax.all_to_all(jnp.stack(jnp.split(keys, lax.axis_size("head"), axis=1)), "head", 0, 0),
+            axis=0,
+        ),
         lax.all_to_all(values, "head", split_axis=1, concat_axis=0, tiled=True),
     )
     whole_keys, whole_values = (whole_of(local_keys, SEQ, 0), whole_of(local_values, SEQ, 0))

time: 249 us -> 254 us (1.020)
  local copies, waits for them, and re-layouts: 3.2 us -> 7.29 us
    unnamed x16 -> x23, local copies, waits for them, and re-layouts: 2.07 us -> 6.3 us
  transfers between devices with their start and end apart: 4 -> 4, of which waited for: 1 -> 1; matrix products, arithmetic and copies ran while one was open for 4% -> 3% of each run, Pallas kernels for 0% -> 0%
where the time goes in v1:
time: 254 us; the launch traced here: 252 us
  blocking collectives  151 us (59%)
  matrix products  41.5 us (16%)
  waiting for transfers between devices  34.9 us (14%)
  between operations  14 us (6%)
  local copies, waits for them, and re-layouts  7.29 us (3%)
    all_gather x1, blocking collectives, gather_packed(): lines, at, gathered = (lax.all_gather(ravelled, axis), 0, [])  80.2 us
    all_gather x4, blocking collectives, whole_of(): filled = lax.all_gather(filled, axes[number], axis=dim, tiled=True)  53.9 us
    all_gather x4, waiting for transfers between devices, whole_of(): filled = lax.all_gather(filled, axes[number], axis=dim, tiled=True)  34.8 us
    dot_general x8, matrix products, key_compute(): jnp.einsum('qk,qd->kd', grad_scores, query_piece, preferred_element_type=...  13.6 us
    dot_general x8, matrix products, key_compute(): jnp.einsum('qd,kd->qk', query_piece, own_keys, preferred_element_type=jnp...  10.9 us
    dot_general x8, matrix products, key_compute(): jnp.einsum('qk,qd->kd', probs.astype(jnp.bfloat16), grad_piece, preferred...  10.4 us
    all_to_all x1, blocking collectives, per_device(): lax.all_to_all(jnp.stack(jnp.split(keys, lax.axis_size('head'), axis=1)),...  8.87 us
    all_to_all x1, blocking collectives, per_device(): lax.all_to_all(values, 'head', split_axis=1, concat_axis=0, tiled=True)  8 us
  transfers between devices with their start and end apart: 4, of which 1 were waited for; matrix products, arithmetic and copies ran while one was open for 3% of the time, Pallas kernels for 0%

profile of v1, /device:TPU:8, one launch (start us, length us, event | category | flops | bytes accessed | tf_op | source)
XLA Modules:
  0.0 252.4 jit_solution(7943227475381176916)
XLA Ops:
  13.0 8.9 %all_to_all.24 = bf16[8,32,128]{2,1,0:T(8,128)(2,1)S(1)} all-to-all(bf16[8,32,128]{2,1,0:T(8,128)(2,1)S(1)} %constant_dynamic-update-slice_fusion), channel_id=1, replica_groups=mesh['seq_0'=8,'seq_1'=4,'head'=8] {'head'}, dimensions={0} | all-to-all | bytes 131072 | tf_op jit(solution)/shard_map/all_to_all | solution.py:200
  21.8 13.3 %all_gather.30 = bf16[1024,128]{1,0:T(8,128)(2,1)} all-gather(bf16[256,128]{1,0:T(8,128)(2,1)S(1)} %bitcast.62), channel_id=1, replica_groups=mesh['seq_0'=8,'seq_1'=4,'head'=8] {'seq_1'}, dimensions={0}, use_global_device_ids=true | all-gather | bytes 327680 | tf_op jit(solution)/shard_map/all_gather | solution.py:16
  35.3 8.0 %all_to_all.25 = bf16[32,8,128]{2,0,1:T(8,128)(2,1)S(1)} all-to-all(bf16[32,8,128]{2,0,1:T(8,128)(2,1)S(1)} %copy_bitcast_fusion), channel_id=1, replica_groups=mesh['seq_0'=8,'seq_1'=4,'head'=8] {'head'}, dimensions={1} | all-to-all | bytes 131072 | tf_op jit(solution)/shard_map/all_to_all | solution.py:203
  43.3 13.0 %all_gather.32 = bf16[1024,128]{1,0:T(8,128)(2,1)} all-gather(bf16[256,128]{1,0:T(8,128)(2,1)S(1)} %bitcast.60), channel_id=1, replica_groups=mesh['seq_0'=8,'seq_1'=4,'head'=8] {'seq_1'}, dimensions={0}, use_global_device_ids=true | all-gather | bytes 327680 | tf_op jit(solution)/shard_map/all_gather | solution.py:16
  56.3 14.3 %all_gather.34 = bf16[1024,128]{1,0:T(8,128)(2,1)} all-gather(bf16[256,128]{1,0:T(8,128)(2,1)} %param.16), channel_id=1, replica_groups=mesh['seq_0'=8,'seq_1'=4,'head'=8] {'seq_1'}, dimensions={0}, use_global_device_ids=true | all-gather | bytes 327680 | tf_op jit(solution)/shard_map/all_gather | solution.py:16
  70.7 13.3 %all_gather.38 = bf16[1024,128]{1,0:T(8,128)(2,1)} all-gather(bf16[256,128]{1,0:T(8,128)(2,1)S(1)} %copy-done.4), channel_id=1, replica_groups=mesh['seq_0'=8,'seq_1'=4,'head'=8] {'seq_1'}, dimensions={0}, use_global_device_ids=true | all-gather | bytes 327680 | tf_op jit(solution)/shard_map/all_gather | solution.py:16
  84.0 34.8 %all-gather.9.cloned.1.call-done = bf16[8192,128]{1,0:T(8,128)(2,1)} async-done(((bf16[1024,128]{1,0:T(8,128)(2,1)}), bf16[8192,128]{1,0:T(8,128)(2,1)}) %all-gather.9.cloned.1.call-update) | async-done | bytes 2097168 | tf_op jit(solution)/shard_map/all_gather | solution.py:16
  118.9 5.1 %while.56 = (s32[]{:T(128)}, f32[256,128]{1,0:T(8,128)S(1)}, f32[256]{0:T(256)S(1)}, f32[256]{0:T(256)S(1)}, s32[]{:T(128)}, /*index=5*/bf16[8192,128]{1,0:T(8,1...) while((s32[]{:T(128)}, f32[256,128]{1,0:T(8,128)S(1)}, ...), condition=%wide.region_5.6_spmd.clone, body=%wide.region_0.5_spmd.clone.sunk | while | flops 139006736 | bytes 4045177 | solution.py:87
  118.9 4.6 %conditional.10 = ((f32[256,128]{1,0:T(8,128)S(1)}, f32[256]{0:T(256)S(1)}, f32[256]{0:T(256)S(1)})) conditional(s32[]{:T(128)} %convert_element_type.68, (f32[256,128]{1,0:T(8,128)S(1)}, f32[256]{0:T(256)S(1)}, f32[256]{0:T(256)S(1)}) %tuple.146, (s32[]{:T(128)}, s32[]{:T(128)}, bf16[8192,128]{1,0:T(8,128)(2,1)}, bf16[256,128]{1,0:T(8,128)(2,1)S(1)}, ...), branch_computations={%region_1.0_spmd, %region_2.4_spmd} | conditional | flops 139006720 | bytes 4043862 | solution.py:75
  119.0 1.9 fusion.68
  121.7 1.8 convolution_add_fusion
  124.8 80.2 %all-gather.1 = f32[32,1,512]{2,1,0:T(1,128)S(1)} all-gather(f32[1,1,512]{2,1,0:T(1,128)S(1)} %bitcast.67), channel_id=2, replica_groups=mesh['seq_0'=8,'seq_1'=4,'head'=8] {'seq_0','seq_1'}, dimensions={0}, use_global_device_ids=true | all-gather | bytes 67584 | tf_op jit(solution)/shard_map/all_gather | solution.py:28
  205.0 3.5 %while.57 = (s32[]{:T(128)}, f32[256,128]{1,0:T(8,128)S(1)}, s32[]{:T(128)}, bf16[8192,128]{1,0:T(8,128)(2,1)}, bf16[256,128]{1,0:T(8,128)(2,1)S(1)}, /*index=5*...) while((s32[]{:T(128)}, f32[256,128]{1,0:T(8,128)S(1)}, ...), condition=%wide.region_10.11_spmd.clone, body=%wide.region_7.10_spmd.clone.sunk | while | flops 203985168 | bytes 3296597 | solution.py:144
  205.1 3.0 %conditional.11 = (f32[256,128]{1,0:T(8,128)S(1)}) conditional(s32[]{:T(128)} %convert_element_type.69, f32[256,128]{1,0:T(8,128)S(1)} %get-tuple-element.1194, (s32[]{:T(128)}, s32[]{:T(128)}, bf16[8192,128]{1,0:T(8,128)(2,1)}, bf16[256,128]{1,0:T(8,128)(2,1)S(1)}, f32[256]{0:T(256)S(1)}, /*index=5*/bf16[8192,128]{1,0:T(8,128)(2,1)}, ...), branch_computations={%region_8.8_spmd, %region_9.9_spmd} | conditional | flops 203985152 | bytes 3295290 | solution.py:136
  209.2 35.9 %while.58 = (s32[]{:T(128)}, f32[256,128]{1,0:T(8,128)S(1)}, f32[256,128]{1,0:T(8,128)S(1)}, s32[]{:T(128)}, bf16[8192,128]{1,0:T(8,128)(2,1)}, /*index=5*/bf16[...) while((s32[]{:T(128)}, f32[256,128]{1,0:T(8,128)S(1)}, ...), condition=%wide.region_14.15_spmd.clone.clone, body=%wide.region_11.14_spmd.clone.clone.sunk | while | flops 270861568 | bytes 4887901 | solution.py:192
  209.2 4.4 %conditional.12 = ((f32[256,128]{1,0:T(8,128)S(1)}, f32[256,128]{1,0:T(8,128)S(1)})) conditional(s32[]{:T(128)} %convert_element_type.70, (f32[256,128]{1,0:T(8,128)S(1)}, f32[256,128]{1,0:T(8,128)S(1)}) %tuple.151, (s32[]{:T(128)}, s32[]{:T(128)}, bf16[8192,128]{1,0:T(8,128)(2,1)}, bf16[256,128]{1,0:T(8,128)(2,1)S(1)}, f32[8192]{0:T(1024)S(1)}, ...), branch_computations={%region_12.12_spmd, %region_13.13_spmd} | conditional | flops 270861568 | bytes 4886610 | solution.py:181
  213.6 4.5 %conditional.12 = ((f32[256,128]{1,0:T(8,128)S(1)}, f32[256,128]{1,0:T(8,128)S(1)})) conditional(s32[]{:T(128)} %convert_element_type.70, (f32[256,128]{1,0:T(8,128)S(1)}, f32[256,128]{1,0:T(8,128)S(1)}) %tuple.151, (s32[]{:T(128)}, s32[]{:T(128)}, bf16[8192,128]{1,0:T(8,128)(2,1)}, bf16[256,128]{1,0:T(8,128)(2,1)S(1)}, f32[8192]{0:T(1024)S(1)}, ...), branch_computations={%region_12.12_spmd, %region_13.13_spmd} | conditional | flops 270861568 | bytes 4886610 | solution.py:181
  215.1 1.7 fusion.53
  218.1 4.5 %conditional.12 = ((f32[256,128]{1,0:T(8,128)S(1)}, f32[256,128]{1,0:T(8,128)S(1)})) conditional(s32[]{:T(128)} %convert_element_type.70, (f32[256,128]{1,0:T(8,128)S(1)}, f32[256,128]{1,0:T(8,128)S(1)}) %tuple.151, (s32[]{:T(128)}, s32[]{:T(128)}, bf16[8192,128]{1,0:T(8,128)(2,1)}, bf16[256,128]{1,0:T(8,128)(2,1)S(1)}, f32[8192]{0:T(1024)S(1)}, ...), branch_computations={%region_12.12_spmd, %region_13.13_spmd} | conditional | flops 270861568 | bytes 4886610 | solution.py:181
  222.6 4.5 %conditional.12 = ((f32[256,128]{1,0:T(8,128)S(1)}, f32[256,128]{1,0:T(8,128)S(1)})) conditional(s32[]{:T(128)} %convert_element_type.70, (f32[256,128]{1,0:T(8,128)S(1)}, f32[256,128]{1,0:T(8,128)S(1)}) %tuple.151, (s32[]{:T(128)}, s32[]{:T(128)}, bf16[8192,128]{1,0:T(8,128)(2,1)}, bf16[256,128]{1,0:T(8,128)(2,1)S(1)}, f32[8192]{0:T(1024)S(1)}, ...), branch_computations={%region_12.12_spmd, %region_13.13_spmd} | conditional | flops 270861568 | bytes 4886610 | solution.py:181
  227.1 4.5 %conditional.12 = ((f32[256,128]{1,0:T(8,128)S(1)}, f32[256,128]{1,0:T(8,128)S(1)})) conditional(s32[]{:T(128)} %convert_element_type.70, (f32[256,128]{1,0:T(8,128)S(1)}, f32[256,128]{1,0:T(8,128)S(1)}) %tuple.151, (s32[]{:T(128)}, s32[]{:T(128)}, bf16[8192,128]{1,0:T(8,128)(2,1)}, bf16[256,128]{1,0:T(8,128)(2,1)S(1)}, f32[8192]{0:T(1024)S(1)}, ...), branch_computations={%region_12.12_spmd, %region_13.13_spmd} | conditional | flops 270861568 | bytes 4886610 | solution.py:181
  231.6 4.5 %conditional.12 = ((f32[256,128]{1,0:T(8,128)S(1)}, f32[256,128]{1,0:T(8,128)S(1)})) conditional(s32[]{:T(128)} %convert_element_type.70, (f32[256,128]{1,0:T(8,128)S(1)}, f32[256,128]{1,0:T(8,128)S(1)}) %tuple.151, (s32[]{:T(128)}, s32[]{:T(128)}, bf16[8192,128]{1,0:T(8,128)(2,1)}, bf16[256,128]{1,0:T(8,128)(2,1)S(1)}, f32[8192]{0:T(1024)S(1)}, ...), branch_computations={%region_12.12_spmd, %region_13.13_spmd} | conditional | flops 270861568 | bytes 4886610 | solution.py:181
  236.1 4.5 %conditional.12 = ((f32[256,128]{1,0:T(8,128)S(1)}, f32[256,128]{1,0:T(8,128)S(1)})) conditional(s32[]{:T(128)} %convert_element_type.70, (f32[256,128]{1,0:T(8,128)S(1)}, f32[256,128]{1,0:T(8,128)S(1)}) %tuple.151, (s32[]{:T(128)}, s32[]{:T(128)}, bf16[8192,128]{1,0:T(8,128)(2,1)}, bf16[256,128]{1,0:T(8,128)(2,1)S(1)}, f32[8192]{0:T(1024)S(1)}, ...), branch_computations={%region_12.12_spmd, %region_13.13_spmd} | conditional | flops 270861568 | bytes 4886610 | solution.py:181
  240.6 4.5 %conditional.12 = ((f32[256,128]{1,0:T(8,128)S(1)}, f32[256,128]{1,0:T(8,128)S(1)})) conditional(s32[]{:T(128)} %convert_element_type.70, (f32[256,128]{1,0:T(8,128)S(1)}, f32[256,128]{1,0:T(8,128)S(1)}) %tuple.151, (s32[]{:T(128)}, s32[]{:T(128)}, bf16[8192,128]{1,0:T(8,128)(2,1)}, bf16[256,128]{1,0:T(8,128)(2,1)S(1)}, f32[8192]{0:T(1024)S(1)}, ...), branch_computations={%region_12.12_spmd, %region_13.13_spmd} | conditional | flops 270861568 | bytes 4886610 | solution.py:181
  (150 shorter events, 45.6 us)
Async XLA Ops:
  7.2 28.1 %copy-start = (bf16[32,1024]{1,0:T(8,128)(2,1)S(1)}, bf16[32,1024]{1,0:T(8,128)(2,1)}, u32[]{:S(2)}) copy-start(bf16[32,1024]{1,0:T(8,128)(2,1)} %param.18) | copy-start | bytes 196612
  7.2 111.7 %copy-start.5 = (bf16[256,128]{1,0:T(8,128)(2,1)S(1)}, bf16[256,128]{1,0:T(8,128)(2,1)}, u32[]{:S(2)}) copy-start(bf16[256,128]{1,0:T(8,128)(2,1)} %param.16) | copy-start | bytes 196612
  7.2 63.5 %copy-start.4 = (bf16[256,128]{1,0:T(8,128)(2,1)S(1)}, bf16[256,128]{1,0:T(8,128)(2,1)}, u32[]{:S(2)}) copy-start(bf16[256,128]{1,0:T(8,128)(2,1)} %param.19) | copy-start | bytes 196612
  7.2 76.8 %all-gather.7.cloned.1.call-start = ((), (), s32[]{:S(2)}) async-start(), calls=%async_computation.2 | async-start | bytes 2359296 | tf_op jit(solution)/shard_map/all_gather | solution.py:16
  35.2 83.6 %all-gather.9.cloned.1.call-start = ((), (), s32[]{:S(2)}) async-start(), calls=%async_computation.3 | async-start | bytes 2359296 | tf_op jit(solution)/shard_map/all_gather | solution.py:16
  56.3 152.3 %all-gather.11.cloned.1.call-start = ((), (), s32[]{:S(2)}) async-start(), calls=%async_computation.4 | async-start | bytes 2359296 | tf_op jit(solution)/shard_map/all_gather | solution.py:16
  70.7 137.9 %all-gather.13.cloned.1.call-start = ((), (), s32[]{:S(2)}) async-start(), calls=%async_computation.5 | async-start | bytes 2359296 | tf_op jit(solution)/shard_map/all_gather | solution.py:16
  208.5 0.7 copy-start.3
  245.1 0.7 copy-start.1
  245.1 0.7 copy-start.2
Sparse Core Ops, SparseCore 0:
  35.3 42.2 all-gather.6
  79.4 39.4 all-gather.8
  120.6 39.4 all-gather.10
  161.7 39.5 all-gather.12
